TPU v7x, 32 devices: a whole 2x2x4 slice. The times are simulated.
32 devices in a mesh: dp: 4 (over z), head: 8 (over y, x, core).
Axes of the slice: x: 2, y: 2, z: 4, core: 2. Of those that a mesh axis runs over, the one named last changes fastest.
Arguments:
- projected: bfloat16 [12288, 24576], P(('dp', 'head')), may hold values from -64 to 64, as said below
- weight_exp: int32 [12288], P(('dp', 'head')), may hold values from 0 to 3
- damp_exp: int32 [128], replicated, may hold values from 0 to 2
Outputs:
- whitening: float32 [128, 192, 192], P('head')
Inputs may be any that keep to these rules, and one draw needn't show every extreme that they name: `projected`: real values.
All inputs are finite; a program needn't handle non-finite values.
Results may differ from a plain program's by a relative error of at most 0.0003.
Values may be sent and summed in bfloat16 or wider, within the bound.
A program may use at most 192 MiB of HBM per device.

v0:
```python
import jax
import jax.numpy as jnp
from jax import lax
from jax.sharding import PartitionSpec as P

HD = 192


def pack_sym(full):
    size = full.shape[-1]
    half = size // 2
    upper_left = full[..., :half, :half]
    lower_right = full[..., half:, half:]
    lower_left = full[..., half:, :half]
    row_ids = lax.broadcasted_iota(jnp.int32, (half + 1, half), 0)
    col_ids = lax.broadcasted_iota(jnp.int32, (half + 1, half), 1)
    zero_row = jnp.zeros(full.shape[:-2] + (1, half), full.dtype)
    below = jnp.concatenate((zero_row, upper_left), axis=-2)
    above = jnp.concatenate((jnp.swapaxes(lower_right, -1, -2), zero_row), axis=-2)
    top = jnp.where(row_ids > col_ids, below, above)
    return jnp.concatenate((top, lower_left), axis=-2)


def unpack_sym(packed):
    half = packed.shape[-1]
    top = packed[..., : half + 1, :]
    lower_left = packed[..., half + 1 :, :]
    row_ids = lax.broadcasted_iota(jnp.int32, (half, half), 0)
    col_ids = lax.broadcasted_iota(jnp.int32, (half, half), 1)
    first_block = top[..., 1:, :]
    upper_left = jnp.where(row_ids >= col_ids, first_block, jnp.swapaxes(first_block, -1, -2))
    turned = jnp.swapaxes(top[..., :half, :], -1, -2)
    lower_right = jnp.where(row_ids >= col_ids, turned, jnp.swapaxes(turned, -1, -2))
    upper = jnp.concatenate((upper_left, jnp.swapaxes(lower_left, -1, -2)), axis=-1)
    bottom = jnp.concatenate((lower_left, lower_right), axis=-1)
    return jnp.concatenate((upper, bottom), axis=-2)


def encode(grams):
    return pack_sym(grams)


def decode(sent):
    return unpack_sym(sent)


def block_grams(rows, weighted, count):
    left = rows.reshape(rows.shape[0], count, HD)
    right = weighted.reshape(rows.shape[0], count, HD)
    return jnp.einsum("tch,tcg->chg", left, right, preferred_element_type=jnp.float32)


def whiten(grams, damp_exp, first, count):
    exponents = lax.dynamic_slice_in_dim(damp_exp, first, count, 0).astype(jnp.float32)
    size = grams.shape[-1]
    eye = jnp.eye(size, dtype=jnp.float32)
    level = jnp.trace(grams, axis1=1, axis2=2) / size + 1e-06
    damped = grams + (jnp.exp2(-exponents) * level)[:, None, None] * eye
    lower = jnp.linalg.cholesky(damped)

    def invert(factor):
        return jax.scipy.linalg.solve_triangular(factor, eye, lower=True)

    return jax.vmap(invert)(lower)


def on_device(projected, weight_exp, damp_exp):
    n_head = lax.axis_size("head")
    n_dp = lax.axis_size("dp")
    mats = projected.shape[1] // HD
    per_head = mats // n_head
    total = projected.shape[0] * n_head * n_dp
    weights = jnp.exp2(weight_exp.astype(jnp.float32)).astype(jnp.bfloat16)
    scaled = projected * weights[:, None]
    partial_grams = lax.psum_scatter(
        encode(block_grams(projected, scaled, lax.axis_size("head") * per_head) / total),
        "head",
        scatter_dimension=0,
        tiled=True,
    )
    head_base = lax.axis_index("head") * per_head
    share = per_head // n_dp
    owned = lax.psum_scatter(partial_grams, "dp", scatter_dimension=0, tiled=True)
    first = head_base + lax.axis_index("dp") * share
    factors = whiten(decode(owned), damp_exp, first, share)
    return lax.all_gather(factors, "dp", axis=0, tiled=True)


def solution(mesh):
    return jax.shard_map(
        on_device,
        mesh=mesh,
        in_specs=(P(("dp", "head"), None), P(("dp", "head")), P()),
        out_specs=P("head", None, None),
        check_vma=False,
    )
```

profile of v0, /device:TPU:8, one launch (start us, length us, event | category | flops | bytes accessed | tf_op | source)
XLA Modules:
  0.0 525.5 jit_solution(8126503440068038890)
XLA Ops:
  6.6 24.6 %copy.72 = bf16[384,24576]{0,1:T(8,128)(2,1)} copy(bf16[384,24576]{1,0:T(8,128)(2,1)} %param.3) | data formatting | bytes 37748736 | tf_op args[0]
  31.2 16.5 %broadcast_multiply_fusion = bf16[384,24576]{0,1:T(8,128)(2,1)} fusion(bf16[384,24576]{0,1:T(8,128)(2,1)} %copy.72, bf16[384]{0:T(512)(128)(2,1)S(1)} %exponential_convert_fusion), kind=kLoop, calls=%fused_computation.2 | loop fusion | flops 9437184 | bytes 37749504 | tf_op jit(solution)/shard_map/mul | solution.py:74
  47.7 23.7 %multiply_bitcast_fusion = f32[128,192,192]{2,1,0:T(8,128)} fusion(bf16[384,128,192]{0,2,1:T(8,128)(2,1)} %bitcast.42, bf16[384,128,192]{0,2,1:T(8,128)(2,1)} %bitcast.41), kind=kOutput, calls=%fused_computation | convolution fusion | flops 3628597248 | bytes 56623104 | tf_op jit(solution)/shard_map/tch,tcg->chg/dot_general | solution.py:50
  71.4 16.4 %fusion.10 = (f32[128,96,96]{2,1,0:T(8,128)}, f32[128,96,96]{2,1,0:T(8,128)}, f32[128,96,96]{1,2,0:T(8,128)}) fusion(f32[128,192,192]{2,1,0:T(8,128)} %multiply_bitcast_fusion), kind=kLoop, calls=%fused_computation.52 | loop fusion | bytes 28311552 | tf_op jit(solution)/shard_map/slice | solution.py:12
  87.8 6.6 %copy.95 = f32[128,96,96]{1,2,0:T(8,128)} copy(f32[128,96,96]{2,1,0:T(8,128)} %get-tuple-element.25) | data formatting | bytes 9437184
  94.4 9.0 %pad_select_fusion = f32[128,97,96]{1,2,0:T(8,128)} fusion(f32[128,96,96]{1,2,0:T(8,128)} %get-tuple-element.27, f32[128,96,96]{1,2,0:T(8,128)} %copy.95, pred[97,96]{0,1:T(8,128)(4,1)S(1)} %iota_compare_fusion.5), kind=kLoop, calls=%fused_computation.4 | loop fusion | flops 1191936 | bytes 14214240 | tf_op jit(solution)/shard_map/jit(_where)/select_n | solution.py:20
  103.3 8.2 %copy.77 = f32[128,97,96]{2,1,0:T(8,128)} copy(f32[128,97,96]{1,2,0:T(8,128)} %pad_select_fusion) | data formatting | bytes 9535488 | tf_op jit(solution)/shard_map/jit(_where)/select_n | solution.py:20
  111.5 10.5 %pad_maximum_fusion = f32[128,193,96]{2,1,0:T(8,128)} fusion(f32[128,96,96]{2,1,0:T(8,128)} %get-tuple-element.26, f32[128,97,96]{2,1,0:T(8,128)} %copy.77), kind=kLoop, calls=%fused_computation.1 | loop fusion | flops 2371584 | bytes 18972672 | tf_op jit(solution)/shard_map/concatenate | solution.py:21
  122.1 96.0 %reduce-scatter.3.cloned.1.call-done = f32[16,193,96]{2,1,0:T(8,128)} async-done(((f32[128,193,96]{2,1,0:T(8,128)}), f32[16,193,96]{2,1,0:T(8,128)}) %reduce-scatter.3.cloned.1.call-update) | async-done | bytes 1185808 | tf_op jit(solution)/shard_map/reduce_scatter | solution.py:75
  218.8 36.9 %reduce-scatter.5.cloned.1.call-done = f32[4,193,96]{2,1,0:T(8,128)} async-done(((f32[16,193,96]{2,1,0:T(8,128)}), f32[4,193,96]{2,1,0:T(8,128)}) %reduce-scatter.5.cloned.1.call-update) | async-done | bytes 296464 | tf_op jit(solution)/shard_map/reduce_scatter | solution.py:83
  255.6 0.9 slice_bitcast_fusion.4
  256.7 1.2 fusion.11
  258.1 1.0 bitcast_select_fusion
  260.3 46.9 %custom-call.17 = f32[4,128,128]{2,1,0:T(8,128)S(1)} custom-call(f32[4,128,128]{2,1,0:T(8,128)S(1)} %cholesky.126), custom_call_target="Cholesky" | custom-call | tf_op jit(solution)/shard_map/jit(cholesky)/cholesky | solution.py:59
  307.3 39.3 %custom-call.18 = f32[4,1,128,128]{2,3,1,0:T(8,128)S(1)} custom-call(f32[4,1,128,128]{3,2,1,0:T(8,128)S(1)} %get-tuple-element.33), custom_call_target="InvertDiagBlocksLowerTriangular" | custom-call | tf_op jit(solution)/shard_map/jit(cholesky)/cholesky | solution.py:59
  346.6 0.4 constant_dynamic-update-slice_fusion.1
  347.3 23.5 %custom-call.19 = f32[4,64,64]{2,1,0:T(8,128)S(1)} custom-call(f32[4,64,64]{2,1,0:T(8,128)S(1)} %convolution_subtract_fusion.1), custom_call_target="Cholesky" | custom-call | tf_op jit(solution)/shard_map/jit(cholesky)/cholesky | solution.py:59
  371.5 78.6 %custom-call.20 = f32[4,2,128,128]{2,3,1,0:T(8,128)S(1)} custom-call(f32[4,2,128,128]{3,2,1,0:T(8,128)S(1)} %pad_maximum_fusion.2), custom_call_target="InvertDiagBlocksLowerTriangular" | custom-call | tf_op jit(solution)/shard_map/vmap(jit(_solve_triangular))/triangular_solve | solution.py:62
  450.1 0.5 fusion.1
  450.6 0.9 convolution_subtract_fusion
  451.5 0.8 fusion.7
  452.4 1.2 copy.89
  453.6 61.6 %all-gather.2.cloned.1.call-done = f32[16,192,192]{2,1,0:T(8,128)} async-done(((f32[4,192,192]{2,1,0:T(8,128)}), f32[16,192,192]{2,1,0:T(8,128)}) %all-gather.2.cloned.1.call-update) | async-done | bytes 2359312 | tf_op jit(solution)/shard_map/all_gather | solution.py:86
  515.2 3.8 copy.100
  (48 shorter events, 3.3 us)
Async XLA Ops:
  6.5 211.6 %reduce-scatter.3.cloned.1.call-start = ((), (), s32[]{:S(2)}) async-start(), calls=%async_computation.2 | async-start | bytes 14745600 | tf_op jit(solution)/shard_map/reduce_scatter | solution.py:75
  6.6 24.6 %copy-start = (s32[384]{0:T(512)S(1)}, s32[384]{0:T(512)}, u32[]{:S(2)}) copy-start(s32[384]{0:T(512)} %param.4) | copy-start | bytes 4612
  122.0 137.5 %copy-start.1 = (s32[128]{0:T(128)S(1)}, s32[128]{0:T(128)}, u32[]{:S(2)}) copy-start(s32[128]{0:T(128)} %param.5) | copy-start | bytes 1540
  122.1 133.6 %reduce-scatter.5.cloned.1.call-start = ((), (), s32[]{:S(2)}) async-start(), calls=%async_computation.3 | async-start | bytes 2048000 | tf_op jit(solution)/shard_map/reduce_scatter | solution.py:83
  218.1 297.1 %all-gather.2.cloned.1.call-start = ((), (), s32[]{:S(2)}) async-start(), calls=%async_computation.4 | async-start | bytes 3932160 | tf_op jit(solution)/shard_map/all_gather | solution.py:86
Sparse Core Ops, SparseCore 0:
  122.2 95.8 reduce-scatter.2
  220.4 35.2 reduce-scatter.4
  453.7 61.3 all-gather.1
where the time goes:
time: 530 us; the launch traced here: 526 us
  other arithmetic  228 us (43%)
  waiting for transfers between devices  194 us (37%)
  local copies, waits for them, and re-layouts  62.8 us (12%)
  matrix products  26.5 us (5%)
  between operations  13.4 us (3%)
    another operation x10, other arithmetic, whiten(): lower = jnp.linalg.cholesky(damped)  110 us
    reduce_scatter x1, waiting for transfers between devices, on_device(): lax.psum_scatter(encode(block_grams(projected, scaled, lax.axis_size('hea...  96 us
    another operation x8, other arithmetic, invert(): return jax.scipy.linalg.solve_triangular(factor, eye, lower=True)  79.1 us
    all_gather x1, waiting for transfers between devices, on_device(): return lax.all_gather(factors, 'dp', axis=0, tiled=True)  61.6 us
    reduce_scatter x1, waiting for transfers between devices, on_device(): lax.psum_scatter(partial_grams, 'dp', scatter_dimension=0, tiled=True)  36.9 us
    unnamed x8, local copies, waits for them, and re-layouts  35.2 us
    dot_general x1, matrix products, block_grams(): jnp.einsum('tch,tcg->chg', left, right, preferred_element_type=jnp.float32)  23.7 us
    mul x1, other arithmetic, on_device(): scaled = projected * weights[:, None]  16.5 us
  transfers between devices with their start and end apart: 3, of which 3 were waited for; matrix products, arithmetic and copies ran while one was open for 0% of the time, Pallas kernels for 0%

commit v1 on v0

v1 whole, which is shorter than its diff:
```python
import functools

import jax
import jax.numpy as jnp
from jax import lax
from jax.experimental import pallas as pl
from jax.experimental.pallas import tpu as pltpu
from jax.sharding import PartitionSpec as P

HD = 192
BLK = HD // 3
HIGH = lax.Precision.HIGHEST


def gram_kernel(rows_ref, weights_ref, out_ref):
    rows = rows_ref[...]
    weighted = rows * weights_ref[...]
    contract = (((0,), (0,)), ((), ()))
    width = 4 * BLK
    first = lax.dot_general(rows[:, :width], weighted[:, :width], contract, preferred_element_type=jnp.float32)
    second = lax.dot_general(rows[:, -width:], weighted[:, -width:], contract, preferred_element_type=jnp.float32)
    two = 2 * BLK
    lanes = lax.broadcasted_iota(jnp.int32, (BLK, two), 1)
    corner = pltpu.roll(first[two : two + BLK, two:], BLK, 1)
    out_ref[0, :BLK, :] = jnp.where(lanes < BLK, first[:BLK, :two], corner)
    out_ref[0, BLK:, :] = first[BLK:HD, :two]
    out_ref[1, :two, :] = second[BLK : BLK + two, two:]
    corner = pltpu.roll(second[BLK:two, :two], BLK, 1)
    out_ref[1, two:, :] = jnp.where(lanes < BLK, corner, second[HD:, two:])


def packed_grams(projected, weights):
    tokens, columns = projected.shape
    mats = columns // HD
    return pl.pallas_call(
        gram_kernel,
        grid=(mats // 2,),
        in_specs=[
            pl.BlockSpec((tokens, 2 * HD), lambda i: (0, i)),
            pl.BlockSpec((tokens, 1), lambda i: (0, 0)),
        ],
        out_specs=pl.BlockSpec((2, HD, 2 * BLK), lambda i: (i, 0, 0)),
        out_shape=jax.ShapeDtypeStruct((mats, HD, 2 * BLK), jnp.float32),
    )(projected, weights)


def dot(a, b):
    return lax.dot_general(a, b, (((1,), (0,)), ((), ())), precision=HIGH, preferred_element_type=jnp.float32)


def dot_t(a, b):
    return lax.dot_general(a, b, (((1,), (1,)), ((), ())), precision=HIGH, preferred_element_type=jnp.float32)


def inverse_factors(blocks):
    lane = lax.broadcasted_iota(jnp.int32, (8, BLK), 1)
    sub = lax.broadcasted_iota(jnp.int32, (8, BLK), 0)
    sub1 = lax.broadcasted_iota(jnp.int32, (8, 1), 0)
    groups = BLK // 8
    held = [[block[8 * g : 8 * g + 8] for g in range(groups)] for block in blocks]
    for k in range(BLK):
        own, spot = divmod(k, 8)
        is_k = lane == k
        for parts in held:
            row = parts[own][spot : spot + 1, :]
            scale = 1.0 / row[:, k : k + 1]
            row = jnp.where(is_k[:1], 1.0, row) * scale
            for g in range(own, groups):
                part = parts[g]
                column = part[:, k : k + 1]
                if g == own:
                    if spot == 7:
                        continue
                    column = jnp.where(sub1 > spot, column, 0.0)
                    kept = jnp.where(is_k & (sub > spot), 0.0, part)
                else:
                    kept = jnp.where(is_k, 0.0, part)
                parts[g] = kept - column * row
    out = []
    for parts in held:
        rows = []
        for g in range(groups):
            ids = sub + 8 * g
            pivot = jnp.sum(jnp.where(lane == ids, parts[g], 0.0), axis=1, keepdims=True)
            unit = jnp.where(lane < ids, parts[g], jnp.where(lane == ids, 1.0, 0.0))
            rows.append(unit * (1.0 / jnp.sqrt(pivot)))
        out.append(jnp.concatenate(rows, axis=0))
    return out


def whiten_kernel(total, count, damp_ref, packed_ref, out_ref):
    two = 2 * BLK
    diag = lax.broadcasted_iota(jnp.int32, (BLK, BLK), 0) == lax.broadcasted_iota(jnp.int32, (BLK, BLK), 1)
    a11, a22, a33, low, a32 = [], [], [], [], []
    for m in range(count):
        got = packed_ref[m] / total
        if m % 2 == 0:
            d1, d3 = got[:BLK, :BLK], got[:BLK, BLK:]
            d2 = got[BLK:two, BLK:]
            left = got[BLK:, :BLK]
            corner = got[two:, BLK:]
        else:
            left = got[:BLK, :].T
            d2 = got[BLK:two, :BLK]
            corner = got[BLK:two, BLK:].T
            d1, d3 = got[two:, :BLK], got[two:, BLK:]
        trace = jnp.sum(jnp.where(diag, d1 + d2 + d3, 0.0), axis=(0, 1), keepdims=True)
        level = trace / HD + 1e-06
        shift = jnp.where(diag, damp_ref[m] * level, 0.0)
        a11.append(d1 + shift)
        a22.append(d2 + shift)
        a33.append(d3 + shift)
        low.append(left)
        a32.append(corner)
    each = range(count)
    w11 = inverse_factors(a11)
    l1 = [dot_t(low[m], w11[m]) for m in each]
    square = [dot_t(l1[m], l1[m]) for m in each]
    w22 = inverse_factors([a22[m] - square[m][:BLK, :BLK] for m in each])
    l32 = [dot_t(a32[m] - square[m][BLK:, :BLK], w22[m]) for m in each]
    w33 = inverse_factors([a33[m] - square[m][BLK:, BLK:] - dot_t(l32[m], l32[m]) for m in each])
    zero = jnp.zeros((BLK, BLK), jnp.float32)
    for m in each:
        below = dot(l1[m], w11[m])
        w21 = -dot(w22[m], below[:BLK])
        w32 = -dot(w33[m], dot(l32[m], w22[m]))
        w31 = -dot(w33[m], below[BLK:] + dot(l32[m], w21))
        out_ref[m, :BLK, :two] = jnp.concatenate((w11[m], zero), axis=1)
        out_ref[m, BLK:two, :two] = jnp.concatenate((w21, w22[m]), axis=1)
        out_ref[m, two:, :two] = jnp.concatenate((w31, w32), axis=1)
        out_ref[m, :two, two:] = jnp.zeros((two, BLK), jnp.float32)
        out_ref[m, two:, two:] = w33[m]


def whiten(packed, damp, total):
    count = packed.shape[0]
    return pl.pallas_call(
        functools.partial(whiten_kernel, total, count),
        in_specs=[pl.BlockSpec(memory_space=pltpu.SMEM), pl.BlockSpec(memory_space=pltpu.VMEM)],
        out_specs=pl.BlockSpec(memory_space=pltpu.VMEM),
        out_shape=jax.ShapeDtypeStruct((count, HD, HD), jnp.float32),
    )(damp, packed)


def on_device(projected, weight_exp, damp_exp):
    n_head = lax.axis_size("head")
    n_dp = lax.axis_size("dp")
    mats = projected.shape[1] // HD
    share = mats // (n_head * n_dp)
    total = projected.shape[0] * n_head * n_dp
    weights = jnp.exp2(weight_exp.astype(jnp.float32)).astype(jnp.bfloat16)
    packed = packed_grams(projected, weights[:, None])
    part = lax.psum_scatter(packed, "head", scatter_dimension=0, tiled=True)
    owned = lax.psum_scatter(part, "dp", scatter_dimension=0, tiled=True)
    first = (lax.axis_index("head") * n_dp + lax.axis_index("dp")) * share
    damp = jnp.exp2(-lax.dynamic_slice_in_dim(damp_exp, first, share, 0).astype(jnp.float32))
    factors = whiten(owned, damp, float(total))
    return lax.all_gather(factors, "dp", axis=0, tiled=True)


def solution(mesh):
    return jax.shard_map(
        on_device,
        mesh=mesh,
        in_specs=(P(("dp", "head"), None), P(("dp", "head")), P()),
        out_specs=P("head", None, None),
        check_vma=False,
    )
```

time: 530 us -> 291 us (0.55)
  other arithmetic: 228 us -> 1.36 us
  Pallas kernels: 0 us -> 75.6 us
  local copies, waits for them, and re-layouts: 62.8 us -> 4.6 us
  matrix products: 26.5 us -> 0 us
    another operation x18 -> x0, other arithmetic: 189 us -> none  [the longest x10 110 us: whiten(): lower = jnp.linalg.cholesky(damped)]
    pallas_call x0 -> x2, Pallas kernels: none -> 75.6 us  [the longest x1 49.6 us: packed_grams(): pl.pallas_call(gram_kernel, grid=(mats // 2,), in_specs=[pl.BlockSpec((to...]
    unnamed x8 -> x3, local copies, waits for them, and re-layouts: 35.2 us -> 3.83 us
    dot_general x1 -> x0, matrix products: 23.7 us -> none  [block_grams(): jnp.einsum('tch,tcg->chg', left, right, preferred_element_type=jnp.float32)]
    mul x2 -> x0, other arithmetic: 16.6 us -> none  [the longest x1 16.5 us: on_device(): scaled = projected * weights[:, None]]
    slice x2 -> x0, local copies, waits for them, and re-layouts: 16.5 us -> none  [the longest x1 16.4 us: pack_sym(): upper_left = full[..., :half, :half]]
    concatenate x2 -> x0, other arithmetic: 10.6 us -> none  [the longest x1 10.5 us: pack_sym(): return jnp.concatenate((top, lower_left), axis=-2)]
    select_n x2 -> x0, other arithmetic: 9.92 us -> none  [the longest x1 8.95 us: pack_sym(): top = jnp.where(row_ids > col_ids, below, above)]
where the time goes in v1:
time: 291 us; the launch traced here: 286 us
  waiting for transfers between devices  191 us (66%)
  Pallas kernels  75.6 us (26%)
  between operations  13.1 us (5%)
  local copies, waits for them, and re-layouts  4.6 us (2%)
    reduce_scatter x1, waiting for transfers between devices, on_device(): part = lax.psum_scatter(packed, 'head', scatter_dimension=0, tiled=True)  93.5 us
    all_gather x1, waiting for transfers between devices, on_device(): return lax.all_gather(factors, 'dp', axis=0, tiled=True)  61.6 us
    pallas_call x1, Pallas kernels, packed_grams(): pl.pallas_call(gram_kernel, grid=(mats // 2,), in_specs=[pl.BlockSpec((to...  49.6 us
    reduce_scatter x1, waiting for transfers between devices, on_device(): owned = lax.psum_scatter(part, 'dp', scatter_dimension=0, tiled=True)  35.7 us
    pallas_call x1, Pallas kernels, whiten(): pl.pallas_call(functools.partial(whiten_kernel, total, count), in_specs=[...  26.1 us
  transfers between devices with their start and end apart: 3, of which 3 were waited for; matrix products, arithmetic and copies ran while one was open for 0% of the time, Pallas kernels for 0%

profile of v1, /device:TPU:8, one launch (start us, length us, event | category | flops | bytes accessed | tf_op | source)
XLA Modules:
  0.0 285.6 jit_solution(10368548867840172545)
XLA Ops:
  6.5 0.0 reduce-scatter.3.cloned.1.call-start
  6.5 0.7 exponential_convert_fusion
  7.2 0.8 broadcast_in_dim.4.weights_ref
  8.0 49.6 %shard_map.37 = f32[128,192,128]{2,1,0:T(8,128)} custom-call(bf16[384,24576]{1,0:T(8,128)(2,1)} %rows_ref.1, bf16[384,1]{1,0:T(8,128)(2,1)} %broadcast_in_dim.4.weights_ref), custom_call_target="tpu_custom_call" | custom-call | tf_op jit(solution)/shard_map/pallas_call | solution.py:35
  57.6 0.0 copy-start
  57.6 0.0 reduce-scatter.3.cloned.1.call-update
  57.6 0.0 reduce-scatter.5.cloned.1.call-start
  57.6 93.5 %reduce-scatter.3.cloned.1.call-done = f32[16,192,128]{2,1,0:T(8,128)} async-done(((f32[128,192,128]{2,1,0:T(8,128)}), f32[16,192,128]{2,1,0:T(8,128)}) %reduce-scatter.3.cloned.1.call-update) | async-done | bytes 1572880 | tf_op jit(solution)/shard_map/reduce_scatter | solution.py:153
  151.2 0.0 reduce-scatter.5.cloned.1.call-update
  151.2 0.0 all-gather.2.cloned.1.call-start
  151.3 0.0 copy-done
  151.3 0.7 multiply_exponential_fusion.damp_ref
  151.9 35.7 %reduce-scatter.5.cloned.1.call-done.packed_ref = f32[4,192,128]{2,1,0:T(8,128)} async-done(((f32[16,192,128]{2,1,0:T(8,128)}), f32[4,192,128]{2,1,0:T(8,128)}) %reduce-scatter.5.cloned.1.call-update) | async-done | bytes 393232 | tf_op jit(solution)/shard_map/reduce_scatter | solution.py:154
  187.6 26.1 %shard_map.38 = f32[4,192,192]{2,1,0:T(8,128)} custom-call(f32[4]{0:T(128)} %multiply_exponential_fusion.damp_ref, f32[4,192,128]{2,1,0:T(8,128)} %reduce-scatter.5.cloned.1.call-done.packed_ref), custom_call_target="tpu_custom_call" | custom-call | tf_op jit(solution)/shard_map/pallas_call | solution.py:137
  213.7 0.0 all-gather.2.cloned.1.call-update
  213.7 61.6 %all-gather.2.cloned.1.call-done = f32[16,192,192]{2,1,0:T(8,128)} async-done(((f32[4,192,192]{2,1,0:T(8,128)}), f32[16,192,192]{2,1,0:T(8,128)}) %all-gather.2.cloned.1.call-update) | async-done | bytes 2359312 | tf_op jit(solution)/shard_map/all_gather | solution.py:158
  275.3 3.8 %copy.7 = f32[16,192,192]{2,1,0:T(8,128)} copy(f32[16,192,192]{2,1,0:T(8,128)} %all-gather.2.cloned.1.call-done) | data formatting | bytes 4718592
Async XLA Ops:
  6.5 144.6 %reduce-scatter.3.cloned.1.call-start = ((), (), s32[]{:S(2)}) async-start(), calls=%async_computation.2 | async-start | bytes 14155776 | tf_op jit(solution)/shard_map/reduce_scatter | solution.py:153
  57.6 93.7 %copy-start = (s32[128]{0:T(128)S(1)}, s32[128]{0:T(128)}, u32[]{:S(2)}) copy-start(s32[128]{0:T(128)} %param.5) | copy-start | bytes 1540
  57.6 130.0 %reduce-scatter.5.cloned.1.call-start = ((), (), s32[]{:S(2)}) async-start(), calls=%async_computation.3 | async-start | bytes 1966080 | tf_op jit(solution)/shard_map/reduce_scatter | solution.py:154
  151.2 124.1 %all-gather.2.cloned.1.call-start = ((), (), s32[]{:S(2)}) async-start(), calls=%async_computation.4 | async-start | bytes 3932160 | tf_op jit(solution)/shard_map/all_gather | solution.py:158
Sparse Core Ops, SparseCore 0:
  57.7 93.4 reduce-scatter.2
  153.5 34.0 reduce-scatter.4
  213.8 61.4 all-gather.1

commit v2 on v1

--- a/solution.py
+++ b/solution.py
@@ -88,22 +88,29 @@
     return out
 
 
+def unpack_even(got):
+    two = 2 * BLK
+    return got[:BLK, :BLK], got[BLK:two, BLK:], got[:BLK, BLK:], got[BLK:, :BLK], got[two:, BLK:]
+
+
+def unpack_odd(got):
+    two = 2 * BLK
+    return got[two:, :BLK], got[BLK:two, :BLK], got[two:, BLK:], got[:BLK, :].T, got[BLK:two, BLK:].T
+
+
 def whiten_kernel(total, count, damp_ref, packed_ref, out_ref):
     two = 2 * BLK
     diag = lax.broadcasted_iota(jnp.int32, (BLK, BLK), 0) == lax.broadcasted_iota(jnp.int32, (BLK, BLK), 1)
     a11, a22, a33, low, a32 = [], [], [], [], []
     for m in range(count):
         got = packed_ref[m] / total
-        if m % 2 == 0:
-            d1, d3 = got[:BLK, :BLK], got[:BLK, BLK:]
-            d2 = got[BLK:two, BLK:]
-            left = got[BLK:, :BLK]
-            corner = got[two:, BLK:]
+        even = unpack_even(got)
+        odd = unpack_odd(got)
+        if count % 2 == 0:
+            d1, d2, d3, left, corner = odd if m % 2 else even
         else:
-            left = got[:BLK, :].T
-            d2 = got[BLK:two, :BLK]
-            corner = got[BLK:two, BLK:].T
-            d1, d3 = got[two:, :BLK], got[two:, BLK:]
+            turn = (lax.axis_index("head") * lax.axis_size("dp") + lax.axis_index("dp")) * count + m
+            d1, d2, d3, left, corner = (jnp.where(turn % 2 == 0, a, b) for a, b in zip(even, odd))
         trace = jnp.sum(jnp.where(diag, d1 + d2 + d3, 0.0), axis=(0, 1), keepdims=True)
         level = trace / HD + 1e-06
         shift = jnp.where(diag, damp_ref[m] * level, 0.0)
@@ -119,17 +126,14 @@
     w22 = inverse_factors([a22[m] - square[m][:BLK, :BLK] for m in each])
     l32 = [dot_t(a32[m] - square[m][BLK:, :BLK], w22[m]) for m in each]
     w33 = inverse_factors([a33[m] - square[m][BLK:, BLK:] - dot_t(l32[m], l32[m]) for m in each])
-    zero = jnp.zeros((BLK, BLK), jnp.float32)
     for m in each:
         below = dot(l1[m], w11[m])
         w21 = -dot(w22[m], below[:BLK])
         w32 = -dot(w33[m], dot(l32[m], w22[m]))
         w31 = -dot(w33[m], below[BLK:] + dot(l32[m], w21))
-        out_ref[m, :BLK, :two] = jnp.concatenate((w11[m], zero), axis=1)
-        out_ref[m, BLK:two, :two] = jnp.concatenate((w21, w22[m]), axis=1)
-        out_ref[m, two:, :two] = jnp.concatenate((w31, w32), axis=1)
-        out_ref[m, :two, two:] = jnp.zeros((two, BLK), jnp.float32)
-        out_ref[m, two:, two:] = w33[m]
+        out_ref[m, :BLK] = jnp.concatenate((w11[m], w33[m]), axis=1)
+        out_ref[m, BLK:two] = jnp.concatenate((w21, w22[m]), axis=1)
+        out_ref[m, two:] = jnp.concatenate((w31, w32), axis=1)
 
 
 def whiten(packed, damp, total):
@@ -138,8 +142,223 @@
         functools.partial(whiten_kernel, total, count),
         in_specs=[pl.BlockSpec(memory_space=pltpu.SMEM), pl.BlockSpec(memory_space=pltpu.VMEM)],
         out_specs=pl.BlockSpec(memory_space=pltpu.VMEM),
-        out_shape=jax.ShapeDtypeStruct((count, HD, HD), jnp.float32),
+        out_shape=jax.ShapeDtypeStruct(packed.shape, jnp.float32),
     )(damp, packed)
+
+
+def flip(index, step):
+    return index + step * (1 - 2 * ((index // step) % 2))
+
+
+def remote(src, dst, sems, slot, device):
+    return pltpu.make_async_remote_copy(
+        src_ref=src,
+        dst_ref=dst,
+        send_sem=sems.at[0, slot],
+        recv_sem=sems.at[1, slot],
+        device_id=device,
+        device_id_type=pl.DeviceIdType.MESH,
+    )
+
+
+def greet(heads, dps):
+    barrier = pltpu.get_barrier_semaphore()
+    for peer in heads:
+        pl.semaphore_signal(barrier, inc=1, device_id={"head": peer}, device_id_type=pl.DeviceIdType.MESH)
+    for peer in dps:
+        pl.semaphore_signal(barrier, inc=1, device_id={"dp": peer}, device_id_type=pl.DeviceIdType.MESH)
+    pl.semaphore_wait(barrier, len(heads) + len(dps))
+
+
+def part_rows():
+    last = HD // 4
+    first = (HD - last) // 2
+    return (0, first), (first, first), (2 * first, last)
+
+
+def scatter_kernel(n_head, n_dp, share, packed_ref, out_ref, acc, got_a, got_b, got_c, got_z, got_y, sem_0, sem_a, sem_b, sem_c, sem_z, sem_y):
+    head = lax.axis_index("head")
+    dp = lax.axis_index("dp")
+    chunks = n_head // 2
+    bits = chunks.bit_length() - 1
+    mine = head // 2
+    core = head % 2
+    per_head = share * n_dp
+    peers = [lax.rem(dp + o, n_dp) for o in range(1, n_dp)]
+    greet([flip(head, 1 << j) for j in range(bits + 1)], peers)
+
+    pair = []
+    for c in range(chunks):
+        theirs = (2 * c + 1 - core) * per_head
+        copy = remote(packed_ref.at[pl.ds(theirs, per_head)], acc.at[c], sem_0, c, {"head": flip(head, 1)})
+        copy.start()
+        pair.append(copy)
+    for c in range(chunks):
+        pair[c].wait()
+        base = (2 * c + core) * per_head
+
+        def add(m, carry, c=c, base=base):
+            acc[c, m] += packed_ref[base + m]
+            return carry
+
+        lax.fori_loop(0, per_head, add, 0)
+
+    def begin(part, got, sems, order, step, first, count):
+        j = order[step]
+        bit = (mine // (1 << j)) % 2
+        fixed = 0
+        for done in order[:step]:
+            fixed = fixed + (mine // (1 << done)) % 2 * (1 << done)
+        free = [b for b in range(bits) if b not in order[: step + 1]]
+        flight = []
+        start, size = part
+        offset = sum(chunks >> (s + 1) for s in range(step))
+        for e in range(1 << len(free)):
+            base = fixed + sum(((e >> i) & 1) << b for i, b in enumerate(free))
+            slot = offset + e
+            copy = remote(
+                acc.at[base + (1 - bit) * (1 << j), pl.ds(first, count), pl.ds(start, size)],
+                got.at[slot],
+                sems,
+                slot,
+                {"head": flip(head, 2 << j)},
+            )
+            copy.start()
+            flight.append((copy, base + bit * (1 << j), slot))
+        return flight, part, got, first, count
+
+    def finish(state):
+        flight, (start, size), got, first, count = state
+        for copy, keep, slot in flight:
+            copy.wait()
+
+            def add(m, carry, keep=keep, slot=slot):
+                acc[keep, first + m, start : start + size] += got[slot, m]
+                return carry
+
+            lax.fori_loop(0, count, add, 0)
+
+    part_a, part_b, part_c = part_rows()
+    up = list(range(bits))
+    down = up[::-1]
+    rows_c = pl.ds(part_c[0], part_c[1])
+    own = dp * share
+    flight_z = []
+    for step in range(bits):
+        state_a = begin(part_a, got_a, sem_a, up, step, 0, per_head)
+        state_b = begin(part_b, got_b, sem_b, down, step, 0, per_head)
+        if step == 0:
+            for o, peer in enumerate(peers):
+                copy = remote(acc.at[:, pl.ds(peer * share, share), rows_c], got_z.at[o], sem_z, o, {"dp": peer})
+                copy.start()
+                flight_z.append(copy)
+        finish(state_a)
+        finish(state_b)
+    rows_ab = pl.ds(0, part_c[0])
+    flight_y = []
+    for o, peer in enumerate(peers):
+        copy = remote(acc.at[mine, pl.ds(peer * share, share), rows_ab], got_y.at[o], sem_y, o, {"dp": peer})
+        copy.start()
+        flight_y.append(copy)
+    for copy in flight_z:
+        copy.wait()
+    for c in range(chunks):
+
+        def add_z(m, carry, c=c):
+            value = acc[c, own + m, part_c[0] :]
+            for o in range(len(peers)):
+                value += got_z[o, c, m]
+            acc[c, own + m, part_c[0] :] = value
+            return carry
+
+        lax.fori_loop(0, share, add_z, 0)
+    for step in range(bits):
+        finish(begin(part_c, got_c, sem_c, up, step, own, share))
+    for copy in flight_y:
+        copy.wait()
+
+    def add_y(m, carry):
+        value = acc[mine, own + m, : part_c[0]]
+        for o in range(len(peers)):
+            value += got_y[o, m]
+        out_ref[m, : part_c[0]] = value
+        out_ref[m, part_c[0] :] = acc[mine, own + m, part_c[0] :]
+        return carry
+
+    lax.fori_loop(0, share, add_y, 0)
+
+
+def scatter_sum(packed, n_head, n_dp):
+    mats, rows, lanes = packed.shape
+    per_head = mats // n_head
+    share = per_head // n_dp
+    chunks = n_head // 2
+    (_, rows_a), (_, rows_b), (_, rows_c) = part_rows()
+    f32 = jnp.float32
+    return pl.pallas_call(
+        functools.partial(scatter_kernel, n_head, n_dp, share),
+        in_specs=[pl.BlockSpec(memory_space=pltpu.VMEM)],
+        out_specs=pl.BlockSpec(memory_space=pltpu.VMEM),
+        out_shape=jax.ShapeDtypeStruct((share, rows, lanes), f32),
+        scratch_shapes=[
+            pltpu.VMEM((chunks, per_head, rows, lanes), f32),
+            pltpu.VMEM((chunks - 1, per_head, rows_a, lanes), f32),
+            pltpu.VMEM((chunks - 1, per_head, rows_b, lanes), f32),
+            pltpu.VMEM((chunks - 1, share, rows_c, lanes), f32),
+            pltpu.VMEM((n_dp - 1, chunks, share, rows_c, lanes), f32),
+            pltpu.VMEM((n_dp - 1, share, rows - rows_c, lanes), f32),
+            pltpu.SemaphoreType.DMA((2, chunks)),
+            pltpu.SemaphoreType.DMA((2, chunks - 1)),
+            pltpu.SemaphoreType.DMA((2, chunks - 1)),
+            pltpu.SemaphoreType.DMA((2, chunks - 1)),
+            pltpu.SemaphoreType.DMA((2, n_dp - 1)),
+            pltpu.SemaphoreType.DMA((2, n_dp - 1)),
+        ],
+        compiler_params=pltpu.CompilerParams(collective_id=0, has_side_effects=True, vmem_limit_bytes=60 << 20),
+    )(packed)
+
+
+def gather_kernel(n_dp, share, packed_ref, out_ref, got, sems):
+    dp = lax.axis_index("dp")
+    peers = [lax.rem(dp + o, n_dp) for o in range(1, n_dp)]
+    greet([], peers)
+    flight = []
+    for o, peer in enumerate(peers):
+        copy = remote(packed_ref, got.at[o], sems, o, {"dp": peer})
+        copy.start()
+        flight.append(copy)
+    two = 2 * BLK
+
+    def unpack(source, base):
+        def one(m, carry):
+            top = source[m, :BLK]
+            out_ref[base + m, :BLK, :two] = jnp.where(lax.broadcasted_iota(jnp.int32, (BLK, two), 1) < BLK, top, 0.0)
+            out_ref[base + m, BLK:, :two] = source[m, BLK:]
+            out_ref[base + m, :two, two:] = jnp.zeros((two, BLK), jnp.float32)
+            out_ref[base + m, two:, two:] = top[:, BLK:]
+            return carry
+
+        lax.fori_loop(0, share, one, 0)
+
+    unpack(packed_ref, dp * share)
+    for o in range(n_dp - 1):
+        flight[o].wait()
+        unpack(got.at[o], lax.rem(dp + n_dp - 1 - o, n_dp) * share)
+
+
+def gather(packed, n_dp):
+    share, rows, lanes = packed.shape
+    return pl.pallas_call(
+        functools.partial(gather_kernel, n_dp, share),
+        in_specs=[pl.BlockSpec(memory_space=pltpu.VMEM)],
+        out_specs=pl.BlockSpec(memory_space=pltpu.VMEM),
+        out_shape=jax.ShapeDtypeStruct((n_dp * share, HD, HD), jnp.float32),
+        scratch_shapes=[
+            pltpu.VMEM((n_dp - 1, share, rows, lanes), jnp.float32),
+            pltpu.SemaphoreType.DMA((2, n_dp - 1)),
+        ],
+        compiler_params=pltpu.CompilerParams(collective_id=1, has_side_effects=True),
+    )(packed)
 
 
 def on_device(projected, weight_exp, damp_exp):
@@ -150,12 +369,11 @@
     total = projected.shape[0] * n_head * n_dp
     weights = jnp.exp2(weight_exp.astype(jnp.float32)).astype(jnp.bfloat16)
     packed = packed_grams(projected, weights[:, None])
-    part = lax.psum_scatter(packed, "head", scatter_dimension=0, tiled=True)
-    owned = lax.psum_scatter(part, "dp", scatter_dimension=0, tiled=True)
+    owned = scatter_sum(packed, n_head, n_dp)
     first = (lax.axis_index("head") * n_dp + lax.axis_index("dp")) * share
     damp = jnp.exp2(-lax.dynamic_slice_in_dim(damp_exp, first, share, 0).astype(jnp.float32))
     factors = whiten(owned, damp, float(total))
-    return lax.all_gather(factors, "dp", axis=0, tiled=True)
+    return gather(factors, n_dp)
 
 
 def solution(mesh):

time: 291 us -> 211 us (0.73); the launches traced: 286 us -> 209 us
  waiting for transfers between devices: 191 us -> 0 us
  Pallas kernels: 75.6 us -> 203 us
  between operations: 13.1 us -> 0.02 us
    reduce_scatter x2 -> x0, waiting for transfers between devices: 129 us -> none  [the longest x1 93.5 us: on_device(): part = lax.psum_scatter(packed, 'head', scatter_dimension=0, tiled=True)]
    pallas_call x0 -> x2, Pallas kernels: none -> 127 us  [the longest x1 87.7 us: scatter_sum(): pl.pallas_call(functools.partial(scatter_kernel, n_head, n_dp, share), in...]
    all_gather x1 -> x0, waiting for transfers between devices: 61.6 us -> none  [on_device(): return lax.all_gather(factors, 'dp', axis=0, tiled=True)]
  transfers between devices with their start and end apart: 3 -> 0, of which waited for: 3 -> 0; matrix products, arithmetic and copies ran while one was open for 0% -> 0% of each run, Pallas kernels for 0% -> 0%
where the time goes in v2:
time: 211 us; the launch traced here: 209 us
  Pallas kernels  203 us (96%)
  local copies, waits for them, and re-layouts  4.6 us (2%)
    pallas_call x1, Pallas kernels, scatter_sum(): pl.pallas_call(functools.partial(scatter_kernel, n_head, n_dp, share), in...  87.7 us
    pallas_call x1, Pallas kernels, packed_grams(): pl.pallas_call(gram_kernel, grid=(mats // 2,), in_specs=[pl.BlockSpec((to...  49.6 us
    pallas_call x1, Pallas kernels, gather(): pl.pallas_call(functools.partial(gather_kernel, n_dp, share), in_specs=[p...  39.4 us
    pallas_call x1, Pallas kernels, whiten(): pl.pallas_call(functools.partial(whiten_kernel, total, count), in_specs=[...  25.9 us

profile of v2, /device:TPU:8, one launch (start us, length us, event | category | flops | bytes accessed | tf_op | source)
XLA Modules:
  0.0 209.2 jit_solution(6501989789132505304)
XLA Ops:
  0.0 1.3 multiply_exponential_fusion.damp_ref
  1.3 0.7 exponential_convert_fusion
  2.0 0.8 broadcast_in_dim.4.weights_ref
  2.8 49.6 %shard_map.37.packed_ref = f32[128,192,128]{2,1,0:T(8,128)} custom-call(bf16[384,24576]{1,0:T(8,128)(2,1)} %rows_ref.1, bf16[384,1]{1,0:T(8,128)(2,1)} %broadcast_in_dim.4.weights_ref), custom_call_target="tpu_custom_call" | custom-call | tf_op jit(solution)/shard_map/pallas_call | solution.py:35
  52.3 87.7 %shard_map.38.packed_ref = f32[4,192,128]{2,1,0:T(8,128)} custom-call(f32[128,192,128]{2,1,0:T(8,128)} %shard_map.37.packed_ref), custom_call_target="tpu_custom_call" | custom-call | tf_op jit(solution)/shard_map/pallas_call | solution.py:298
  140.1 25.9 %shard_map.39.packed_ref = f32[4,192,128]{2,1,0:T(8,128)} custom-call(f32[4]{0:T(128)} %multiply_exponential_fusion.damp_ref, f32[4,192,128]{2,1,0:T(8,128)} %shard_map.38.packed_ref), custom_call_target="tpu_custom_call" | custom-call | tf_op jit(solution)/shard_map/pallas_call | solution.py:141
  166.0 39.4 %shard_map.40 = f32[16,192,192]{2,1,0:T(8,128)} custom-call(f32[4,192,128]{2,1,0:T(8,128)} %shard_map.39.packed_ref), custom_call_target="tpu_custom_call" | custom-call | tf_op jit(solution)/shard_map/pallas_call | solution.py:351
  205.4 3.8 %copy.6 = f32[16,192,192]{2,1,0:T(8,128)} copy(f32[16,192,192]{2,1,0:T(8,128)} %shard_map.40) | data formatting | bytes 4718592

commit v3 on v2

--- a/solution.py
+++ b/solution.py
@@ -12,9 +12,8 @@
 HIGH = lax.Precision.HIGHEST
 
 
-def gram_kernel(rows_ref, weights_ref, out_ref):
-    rows = rows_ref[...]
-    weighted = rows * weights_ref[...]
+def store_pair(rows, wide, out, at):
+    weighted = rows * wide
     contract = (((0,), (0,)), ((), ()))
     width = 4 * BLK
     first = lax.dot_general(rows[:, :width], weighted[:, :width], contract, preferred_element_type=jnp.float32)
@@ -22,26 +21,11 @@
     two = 2 * BLK
     lanes = lax.broadcasted_iota(jnp.int32, (BLK, two), 1)
     corner = pltpu.roll(first[two : two + BLK, two:], BLK, 1)
-    out_ref[0, :BLK, :] = jnp.where(lanes < BLK, first[:BLK, :two], corner)
-    out_ref[0, BLK:, :] = first[BLK:HD, :two]
-    out_ref[1, :two, :] = second[BLK : BLK + two, two:]
+    out[at, :BLK, :] = jnp.where(lanes < BLK, first[:BLK, :two], corner)
+    out[at, BLK:, :] = first[BLK:HD, :two]
+    out[at + 1, :two, :] = second[BLK : BLK + two, two:]
     corner = pltpu.roll(second[BLK:two, :two], BLK, 1)
-    out_ref[1, two:, :] = jnp.where(lanes < BLK, corner, second[HD:, two:])
-
-
-def packed_grams(projected, weights):
-    tokens, columns = projected.shape
-    mats = columns // HD
-    return pl.pallas_call(
-        gram_kernel,
-        grid=(mats // 2,),
-        in_specs=[
-            pl.BlockSpec((tokens, 2 * HD), lambda i: (0, i)),
-            pl.BlockSpec((tokens, 1), lambda i: (0, 0)),
-        ],
-        out_specs=pl.BlockSpec((2, HD, 2 * BLK), lambda i: (i, 0, 0)),
-        out_shape=jax.ShapeDtypeStruct((mats, HD, 2 * BLK), jnp.float32),
-    )(projected, weights)
+    out[at + 1, two:, :] = jnp.where(lanes < BLK, corner, second[HD:, two:])
 
 
 def dot(a, b):
@@ -176,7 +160,7 @@
     return (0, first), (first, first), (2 * first, last)
 
 
-def scatter_kernel(n_head, n_dp, share, packed_ref, out_ref, acc, got_a, got_b, got_c, got_z, got_y, sem_0, sem_a, sem_b, sem_c, sem_z, sem_y):
+def scatter_kernel(n_head, n_dp, share, rows_ref, weights_ref, out_ref, acc, sent, own_grams, wide, columns, got_a, got_b, got_c, got_z, got_y, sem_in, sem_0, sem_a, sem_b, sem_c, sem_z, sem_y):
     head = lax.axis_index("head")
     dp = lax.axis_index("dp")
     chunks = n_head // 2
@@ -184,24 +168,77 @@
     mine = head // 2
     core = head % 2
     per_head = share * n_dp
+    span = per_head * HD
     peers = [lax.rem(dp + o, n_dp) for o in range(1, n_dp)]
+    part_a, part_b, part_c = part_rows()
+    up = list(range(bits))
+    down = up[::-1]
+    rows_c = pl.ds(part_c[0], part_c[1])
+
+    def chunk_of(e):
+        chunk = mine
+        for j in range(bits):
+            if (e >> j) & 1:
+                chunk = chunk + (1 - 2 * ((mine // (1 << j)) % 2)) * (1 << j)
+        return chunk
+
+    order = list(range(chunks))[::-1]
+    visits = []
+    for e in order:
+        visits += [2 * chunk_of(e) + 1 - core, 2 * chunk_of(e) + core]
+
+    def fetch(v):
+        start = pl.multiple_of(visits[v] * span, 2 * BLK)
+        return pltpu.make_async_copy(rows_ref.at[:, pl.ds(start, span)], columns.at[v % 2], sem_in.at[v % 2])
+
+    fetch(0).start()
+    wide[...] = jnp.broadcast_to(weights_ref[...], wide.shape)
     greet([flip(head, 1 << j) for j in range(bits + 1)], peers)
 
-    pair = []
-    for c in range(chunks):
-        theirs = (2 * c + 1 - core) * per_head
-        copy = remote(packed_ref.at[pl.ds(theirs, per_head)], acc.at[c], sem_0, c, {"head": flip(head, 1)})
+    def multiply(v, out):
+        if v + 1 < len(visits):
+            fetch(v + 1).start()
+        fetch(v).wait()
+
+        def pair(i, carry):
+            start = pl.multiple_of(i * 2 * HD, 2 * BLK)
+            store_pair(columns[v % 2, :, pl.ds(start, 2 * HD)], wide[...], out, 2 * i)
+            return carry
+
+        lax.fori_loop(0, per_head // 2, pair, 0, unroll=2)
+
+    def squeeze(e, j):
+        return (e >> (j + 1) << j) | (e & ((1 << j) - 1))
+
+    early = {"a": [], "b": []}
+    flight_z = []
+    for n, e in enumerate(order):
+        c = chunk_of(e)
+        multiply(2 * n, sent.at[n])
+        copy = remote(sent.at[n], acc.at[c], sem_0, n, {"head": flip(head, 1)})
         copy.start()
-        pair.append(copy)
-    for c in range(chunks):
-        pair[c].wait()
-        base = (2 * c + core) * per_head
-
-        def add(m, carry, c=c, base=base):
-            acc[c, m] += packed_ref[base + m]
+        multiply(2 * n + 1, own_grams)
+        copy.wait()
+
+        def add(m, carry, c=c):
+            acc[c, m] += own_grams[m]
             return carry
 
         lax.fori_loop(0, per_head, add, 0)
+        for name, (start, size), got, sems, j in (("a", part_a, got_a, sem_a, up[0]), ("b", part_b, got_b, sem_b, down[0])):
+            if (e >> j) & 1:
+                slot = squeeze(e, j)
+                out = remote(
+                    acc.at[c, pl.ds(0, per_head), pl.ds(start, size)], got.at[slot], sems, slot, {"head": flip(head, 2 << j)}
+                )
+                out.start()
+                early[name].append((out, chunk_of(e ^ (1 << j)), slot))
+        for o, peer in enumerate(peers):
+            out = remote(
+                acc.at[c, pl.ds(peer * share, share), rows_c], got_z.at[o, e], sem_z, o * chunks + e, {"dp": peer}
+            )
+            out.start()
+            flight_z.append(out)
 
     def begin(part, got, sems, order, step, first, count):
         j = order[step]
@@ -238,20 +275,14 @@
 
             lax.fori_loop(0, count, add, 0)
 
-    part_a, part_b, part_c = part_rows()
-    up = list(range(bits))
-    down = up[::-1]
-    rows_c = pl.ds(part_c[0], part_c[1])
     own = dp * share
-    flight_z = []
     for step in range(bits):
-        state_a = begin(part_a, got_a, sem_a, up, step, 0, per_head)
-        state_b = begin(part_b, got_b, sem_b, down, step, 0, per_head)
-        if step == 0:
-            for o, peer in enumerate(peers):
-                copy = remote(acc.at[:, pl.ds(peer * share, share), rows_c], got_z.at[o], sem_z, o, {"dp": peer})
-                copy.start()
-                flight_z.append(copy)
+        if step:
+            state_a = begin(part_a, got_a, sem_a, up, step, 0, per_head)
+            state_b = begin(part_b, got_b, sem_b, down, step, 0, per_head)
+        else:
+            state_a = early["a"], part_a, got_a, 0, per_head
+            state_b = early["b"], part_b, got_b, 0, per_head
         finish(state_a)
         finish(state_b)
     rows_ab = pl.ds(0, part_c[0])
@@ -262,12 +293,12 @@
         flight_y.append(copy)
     for copy in flight_z:
         copy.wait()
-    for c in range(chunks):
-
-        def add_z(m, carry, c=c):
+    for e in range(chunks):
+
+        def add_z(m, carry, c=chunk_of(e), e=e):
             value = acc[c, own + m, part_c[0] :]
             for o in range(len(peers)):
-                value += got_z[o, c, m]
+                value += got_z[o, e, m]
             acc[c, own + m, part_c[0] :] = value
             return carry
 
@@ -288,8 +319,9 @@
     lax.fori_loop(0, share, add_y, 0)
 
 
-def scatter_sum(packed, n_head, n_dp):
-    mats, rows, lanes = packed.shape
+def gram_sums(projected, weights, n_head, n_dp):
+    tokens, width = projected.shape
+    mats, rows, lanes = width // HD, HD, 2 * BLK
     per_head = mats // n_head
     share = per_head // n_dp
     chunks = n_head // 2
@@ -297,25 +329,30 @@
     f32 = jnp.float32
     return pl.pallas_call(
         functools.partial(scatter_kernel, n_head, n_dp, share),
-        in_specs=[pl.BlockSpec(memory_space=pltpu.VMEM)],
+        in_specs=[pl.BlockSpec(memory_space=pl.ANY), pl.BlockSpec(memory_space=pltpu.VMEM)],
         out_specs=pl.BlockSpec(memory_space=pltpu.VMEM),
         out_shape=jax.ShapeDtypeStruct((share, rows, lanes), f32),
         scratch_shapes=[
             pltpu.VMEM((chunks, per_head, rows, lanes), f32),
+            pltpu.VMEM((chunks, per_head, rows, lanes), f32),
+            pltpu.VMEM((per_head, rows, lanes), f32),
+            pltpu.VMEM((tokens, 2 * HD), projected.dtype),
+            pltpu.VMEM((2, tokens, per_head * HD), projected.dtype),
             pltpu.VMEM((chunks - 1, per_head, rows_a, lanes), f32),
             pltpu.VMEM((chunks - 1, per_head, rows_b, lanes), f32),
             pltpu.VMEM((chunks - 1, share, rows_c, lanes), f32),
             pltpu.VMEM((n_dp - 1, chunks, share, rows_c, lanes), f32),
             pltpu.VMEM((n_dp - 1, share, rows - rows_c, lanes), f32),
+            pltpu.SemaphoreType.DMA((2,)),
             pltpu.SemaphoreType.DMA((2, chunks)),
             pltpu.SemaphoreType.DMA((2, chunks - 1)),
             pltpu.SemaphoreType.DMA((2, chunks - 1)),
             pltpu.SemaphoreType.DMA((2, chunks - 1)),
-            pltpu.SemaphoreType.DMA((2, n_dp - 1)),
+            pltpu.SemaphoreType.DMA((2, (n_dp - 1) * chunks)),
             pltpu.SemaphoreType.DMA((2, n_dp - 1)),
         ],
         compiler_params=pltpu.CompilerParams(collective_id=0, has_side_effects=True, vmem_limit_bytes=60 << 20),
-    )(packed)
+    )(projected, weights)
 
 
 def gather_kernel(n_dp, share, packed_ref, out_ref, got, sems):
@@ -368,8 +405,7 @@
     share = mats // (n_head * n_dp)
     total = projected.shape[0] * n_head * n_dp
     weights = jnp.exp2(weight_exp.astype(jnp.float32)).astype(jnp.bfloat16)
-    packed = packed_grams(projected, weights[:, None])
-    owned = scatter_sum(packed, n_head, n_dp)
+    owned = gram_sums(projected, weights[:, None], n_head, n_dp)
     first = (lax.axis_index("head") * n_dp + lax.axis_index("dp")) * share
     damp = jnp.exp2(-lax.dynamic_slice_in_dim(damp_exp, first, share, 0).astype(jnp.float32))
     factors = whiten(owned, damp, float(total))

time: 211 us -> 152 us (0.72)
  Pallas kernels: 203 us -> 145 us
    pallas_call x2 -> x1, Pallas kernels: 137 us -> 79.9 us  [gram_sums(): pl.pallas_call(functools.partial(scatter_kernel, n_head, n_dp, share), in...]
where the time goes in v3:
time: 152 us; the launch traced here: 151 us
  Pallas kernels  145 us (95%)
  local copies, waits for them, and re-layouts  4.6 us (3%)
  other arithmetic  2 us (1%)
    pallas_call x1, Pallas kernels, gram_sums(): pl.pallas_call(functools.partial(scatter_kernel, n_head, n_dp, share), in...  79.9 us
    pallas_call x1, Pallas kernels, gather(): pl.pallas_call(functools.partial(gather_kernel, n_dp, share), in_specs=[p...  38.9 us
    pallas_call x1, Pallas kernels, whiten(): pl.pallas_call(functools.partial(whiten_kernel, total, count), in_specs=[...  25.9 us
    unnamed x1, local copies, waits for them, and re-layouts  3.83 us

profile of v3, /device:TPU:8, one launch (start us, length us, event | category | flops | bytes accessed | tf_op | source)
XLA Modules:
  0.0 151.3 jit_solution(17621260722162096797)
XLA Ops:
  0.0 1.3 multiply_exponential_fusion.damp_ref
  1.3 0.7 exponential_convert_fusion
  2.0 0.8 broadcast_in_dim.4.weights_ref
  2.8 79.9 %shard_map.37.packed_ref = f32[4,192,128]{2,1,0:T(8,128)} custom-call(bf16[384,24576]{1,0:T(8,128)(2,1)} %rows_ref.1, bf16[384,1]{1,0:T(8,128)(2,1)} %broadcast_in_dim.4.weights_ref), custom_call_target="tpu_custom_call" | custom-call | tf_op jit(solution)/shard_map/pallas_call | solution.py:330
  82.7 25.9 %shard_map.38.packed_ref = f32[4,192,128]{2,1,0:T(8,128)} custom-call(f32[4]{0:T(128)} %multiply_exponential_fusion.damp_ref, f32[4,192,128]{2,1,0:T(8,128)} %shard_map.37.packed_ref), custom_call_target="tpu_custom_call" | custom-call | tf_op jit(solution)/shard_map/pallas_call | solution.py:125
  108.6 38.9 %shard_map.39 = f32[16,192,192]{2,1,0:T(8,128)} custom-call(f32[4,192,128]{2,1,0:T(8,128)} %shard_map.38.packed_ref), custom_call_target="tpu_custom_call" | custom-call | tf_op jit(solution)/shard_map/pallas_call | solution.py:388
  147.5 3.8 %copy.6 = f32[16,192,192]{2,1,0:T(8,128)} copy(f32[16,192,192]{2,1,0:T(8,128)} %shard_map.39) | data formatting | bytes 4718592
